TPU v7x, 32 devices: a whole 2x2x4 slice. The times are simulated.
32 devices in a mesh: dom: 8 (over z, x), dir: 4 (over y, core).
Axes of the slice: x: 2, y: 2, z: 4, core: 2. Of those that a mesh axis runs over, the one named last changes fastest.
Arguments:
- x_edges: bfloat16 [65536, 128], P(('dom', 'dir')), may hold values from -6 to 6
- send_list: int32 [1024, 32], P(('dom', 'dir')), may hold values from 0 to 2048, as said below
- connectivity: int32 [6, 32768], P(None, ('dom', 'dir')), may hold values from 0 to 3071, as said below
- elem_mats: float32 [36, 32768], P(None, ('dom', 'dir'))
- elem_live: int32 [32], P(('dom', 'dir')), may hold values from 512 to 1024, as said below
- currents: bfloat16 [1024, 128, 128], P(('dom', 'dir')), may hold values from -0.1796875 to 0.1796875
- positions: bfloat16 [1024, 3, 128], P(('dom', 'dir')), may hold values from -1 to 1
- block_live: int32 [1024], P(('dom', 'dir')), may hold values from 32 to 128
- block_owner: int32 [1024], P(('dom', 'dir')), may hold values from 0 to 7, as said below
- block_leaf: int32 [1024], P(('dom', 'dir')), may hold values from 0 to 15
- cone_waves: float32 [3, 16], P(None, 'dir'), may hold values from -6 to 6
Outputs:
- interior_out: float32 [65536, 128], P(('dom', 'dir'))
- expansions: float32 [16, 16, 2, 64, 128], P('dom', 'dir')
Inputs may be any that keep to these rules, and one draw needn't show every extreme that they name: `send_list`: in row a * 32 + b the used entries come first and name owned edges of a; the rest are 2048. A partition reads nothing of itself; some pair uses all 32 entries. `connectivity`: entries below 2048 are owned edges; 2048 + p * 32 + s names the s-th edge that partition p lists for this partition, and only used entries are named. `elem_live`: elements at positions from this count on are padding; some partition has all 1024. `block_owner`: among the 32 blocks of one partition at most 12 name one leaf owner; some leaf owner is named by exactly 12 blocks of every partition.
All inputs are finite; a program needn't handle non-finite values.
Results may differ from a plain program's by a relative error of at most 0.0056.
Values may be sent and summed in bfloat16 or wider, within the bound.
A program may use at most 128 MiB of HBM per device.

v0:
```python
import jax
import jax.numpy as jnp
from jax import lax
from jax.sharding import PartitionSpec as P

LEAVES_DEV = 16
NODES = 4


def cheb_points():
    node_order = jnp.arange(NODES).astype(jnp.float32)
    return jnp.cos((2.0 * node_order + 1.0) * (jnp.pi / (2.0 * NODES)))


def lagrange(points):
    node_values = cheb_points()
    rows_out = []
    for target in range(NODES):
        product = jnp.ones_like(points)
        for other_node in range(NODES):
            if other_node != target:
                product = (
                    product
                    * (points - node_values[other_node])
                    / (node_values[target] - node_values[other_node])
                )
        rows_out.append(product)
    return jnp.stack(rows_out, axis=-2)


def tensor_basis(coords):
    first = lagrange(coords[..., 0, :])
    second = lagrange(coords[..., 1, :])
    third = lagrange(coords[..., 2, :])
    joined = (
        first[..., :, None, None, :] * second[..., None, :, None, :] * third[..., None, None, :, :]
    )
    return joined.reshape(coords.shape[:-2] + (NODES**3, coords.shape[-1]))


def node_coords():
    ladder = jnp.arange(NODES**3)
    digits = jnp.stack([ladder // (NODES * NODES), ladder // NODES % NODES, ladder % NODES]).astype(
        jnp.float32
    )
    return jnp.cos((2.0 * digits + 1.0) * (jnp.pi / (2.0 * NODES)))


def wave_phase(waves, coords):
    return (
        waves[0][:, None] * coords[..., None, 0, :]
        + waves[1][:, None] * coords[..., None, 1, :]
        + waves[2][:, None] * coords[..., None, 2, :]
    )


def m2m_tables(waves):
    octant = jnp.arange(8)
    shifts = jnp.stack([octant // 4, octant // 2 % 2, octant % 2], axis=1).astype(jnp.float32) - 0.5
    points = shifts[:, :, None] + 0.5 * cheb_points()[None, None, :]
    weights = lagrange(points)
    first = weights[:, 0]
    second = weights[:, 1]
    third = weights[:, 2]
    joined = (
        first[:, :, None, None, :, None, None]
        * second[:, None, :, None, None, :, None]
        * third[:, None, None, :, None, None, :]
    )
    square = NODES**3
    joined = joined.reshape(8, square, square)
    child = shifts[:, :, None] + 0.5 * node_coords()[None]
    spread = child[:, :, None, :] - node_coords()[None, :, :, None]
    psi = 2.0 * (
        waves[0][:, None, None, None] * spread[None, :, 0]
        + waves[1][:, None, None, None] * spread[None, :, 1]
        + waves[2][:, None, None, None] * spread[None, :, 2]
    )
    table_real = (joined[None] * jnp.cos(psi)).astype(jnp.bfloat16)
    table_imag = (-joined[None] * jnp.sin(psi)).astype(jnp.bfloat16)
    return (table_real, table_imag)


def pack_slots(owners, dest_count, capacity, members):
    matches = (owners[:, None] == jnp.arange(dest_count)[None, :]).astype(jnp.int32)
    ranking = jnp.sum((jnp.cumsum(matches, axis=0) - matches) * matches, axis=1)
    slot_index = owners * capacity + ranking
    source_row = (
        jnp.full((dest_count * capacity,), owners.shape[0], jnp.int32)
        .at[slot_index]
        .set(jnp.arange(owners.shape[0], dtype=jnp.int32))
    )
    padded = [
        jnp.concatenate([member, jnp.zeros((1,) + member.shape[1:], member.dtype)])
        for member in members
    ]
    return tuple((array_now[source_row] for array_now in padded))


def interior_part(x_edges, send_list, connectivity, elem_mats, elem_live):
    owned_rows, columns = x_edges.shape
    partitions, slot_width = send_list.shape
    element_count = connectivity.shape[1]
    padded = jnp.concatenate([x_edges, jnp.zeros((1, columns), x_edges.dtype)])
    outgoing = padded[send_list]
    received = lax.all_to_all(outgoing, ("dom", "dir"), split_axis=0, concat_axis=0, tiled=True)
    edge_table = jnp.concatenate([x_edges, received.reshape(partitions * slot_width, columns)])
    gathered = edge_table[connectivity]
    live_mask = (jnp.arange(element_count) < elem_live[0])[:, None]
    term_list = []
    for row_index in range(6):
        summed = jnp.zeros((element_count, columns), jnp.float32)
        for col_index in range(6):
            summed = summed + elem_mats[row_index * 6 + col_index][:, None] * gathered[col_index]
        term_list.append(jnp.where(live_mask, summed, jnp.zeros_like(summed)))
    stacked = jnp.stack(term_list).reshape(6 * element_count, columns)
    assembled = jax.ops.segment_sum(
        stacked, connectivity.reshape(-1), num_segments=owned_rows + partitions * slot_width
    )
    back_terms = assembled[owned_rows:]
    returned = lax.all_to_all(
        back_terms.reshape(partitions, slot_width, columns),
        ("dom", "dir"),
        split_axis=0,
        concat_axis=0,
        tiled=True,
    )
    folded = jax.ops.segment_sum(
        returned.reshape(-1, columns), send_list.reshape(-1), num_segments=owned_rows + 1
    )
    return assembled[:owned_rows] + folded[:owned_rows]


def expand_leaves(arrived_blocks, arrived_meta, waves):
    block_size = arrived_blocks.shape[1]
    columns = arrived_blocks.shape[2]
    cone_count = waves.shape[1]
    square = NODES**3
    group_rows = 512 // cone_count
    group_count = arrived_blocks.shape[0] // group_rows
    leaf_ids = arrived_meta[:, 3, 0].astype(jnp.int32)

    def one_group(carry, inputs):
        real_sum, imag_sum = carry
        blocks_now, coords, leaves = inputs
        coords_wide = coords.astype(jnp.float32)
        basis_now = tensor_basis(coords_wide)
        phase_now = wave_phase(waves, coords_wide)
        real_w = (basis_now[:, None] * jnp.cos(phase_now)[:, :, None, :]).astype(jnp.bfloat16)
        imag_w = (-basis_now[:, None] * jnp.sin(phase_now)[:, :, None, :]).astype(jnp.bfloat16)
        real_part = jnp.einsum(
            "gcqb,gbn->gcqn", real_w, blocks_now, preferred_element_type=jnp.float32
        ).astype(jnp.bfloat16)
        imag_part = jnp.einsum(
            "gcqb,gbn->gcqn", imag_w, blocks_now, preferred_element_type=jnp.float32
        ).astype(jnp.bfloat16)
        selector = (jnp.arange(LEAVES_DEV)[:, None] == leaves[None, :]).astype(jnp.bfloat16)
        real_sum = real_sum + jnp.einsum(
            "lg,gcqn->lcqn", selector, real_part, preferred_element_type=jnp.float32
        )
        imag_sum = imag_sum + jnp.einsum(
            "lg,gcqn->lcqn", selector, imag_part, preferred_element_type=jnp.float32
        )
        return ((real_sum, imag_sum), None)

    empty = jnp.zeros((LEAVES_DEV, cone_count, square, columns), jnp.float32)
    inputs = (
        arrived_blocks.reshape(group_count, group_rows, block_size, columns),
        arrived_meta[:, :3].reshape(group_count, group_rows, 3, block_size),
        leaf_ids.reshape(group_count, group_rows),
    )
    sums, unused = lax.scan(one_group, (empty, empty), inputs)
    real_sum, imag_sum = sums
    node_phase = wave_phase(waves, node_coords())
    cosine = jnp.cos(node_phase)[None, :, :, None]
    sine_part = jnp.sin(node_phase)[None, :, :, None]
    leaf_real = (cosine * real_sum - sine_part * imag_sum).astype(jnp.bfloat16)
    leaf_imag = (cosine * imag_sum + sine_part * real_sum).astype(jnp.bfloat16)
    table_real, table_imag = m2m_tables(waves)
    child_real = leaf_real.reshape(LEAVES_DEV // 8, 8, cone_count, square, columns)
    child_imag = leaf_imag.reshape(LEAVES_DEV // 8, 8, cone_count, square, columns)
    parent_real = jnp.einsum(
        "cops,xocsn->xcpn", table_real, child_real, preferred_element_type=jnp.float32
    ) - jnp.einsum("cops,xocsn->xcpn", table_imag, child_imag, preferred_element_type=jnp.float32)
    parent_imag = jnp.einsum(
        "cops,xocsn->xcpn", table_real, child_imag, preferred_element_type=jnp.float32
    ) + jnp.einsum("cops,xocsn->xcpn", table_imag, child_real, preferred_element_type=jnp.float32)
    return jnp.stack([parent_real, parent_imag], axis=2)


def boundary_part(currents, positions, block_live, block_owner, block_leaf, cone_waves):
    block_count, block_size, columns = currents.shape
    dom_count = lax.axis_size("dom")
    capacity = 3 * block_count // dom_count
    live_mask = jnp.arange(block_size)[None, :] < block_live[:, None]
    masked = jnp.where(live_mask[:, :, None], currents, jnp.zeros_like(currents))
    leaf_row = jnp.broadcast_to(
        block_leaf.astype(jnp.bfloat16)[:, None, None], (block_count, 1, block_size)
    )
    described = jnp.concatenate([positions, leaf_row], axis=1)
    packed_blocks, packed_meta = pack_slots(block_owner, dom_count, capacity, (masked, described))
    owner_blocks, owner_meta = (
        lax.all_to_all(packed_blocks, "dom", split_axis=0, concat_axis=0, tiled=True),
        lax.all_to_all(packed_meta, "dom", split_axis=0, concat_axis=0, tiled=True),
    )
    arrived_blocks, arrived_meta = (
        lax.all_gather(owner_blocks, "dir", axis=0, tiled=True),
        lax.all_gather(owner_meta, "dir", axis=0, tiled=True),
    )
    parents = expand_leaves(arrived_blocks, arrived_meta, cone_waves)
    return parents


def shards(
    x_edges,
    send_list,
    connectivity,
    elem_mats,
    elem_live,
    currents,
    positions,
    block_live,
    block_owner,
    block_leaf,
    cone_waves,
):
    interior_out = interior_part(x_edges, send_list, connectivity, elem_mats, elem_live)
    expansions = boundary_part(currents, positions, block_live, block_owner, block_leaf, cone_waves)
    return (interior_out, expansions)


def solution(mesh):
    placed = (
        P(("dom", "dir"), None),
        P(("dom", "dir"), None),
        P(None, ("dom", "dir")),
        P(None, ("dom", "dir")),
        P(("dom", "dir")),
        P(("dom", "dir"), None, None),
        P(("dom", "dir"), None, None),
        P(("dom", "dir")),
        P(("dom", "dir")),
        P(("dom", "dir")),
        P(None, "dir"),
    )
    return jax.shard_map(
        shards,
        mesh=mesh,
        in_specs=placed,
        out_specs=(P(("dom", "dir"), None), P("dom", "dir", None, None, None)),
        check_vma=False,
    )
```

profile of v0, /device:TPU:0, one launch (start us, length us, event | category | flops | bytes accessed | tf_op | source)
XLA Modules:
  0.0 447.4 jit_solution(9750463956113787339)
XLA Ops:
  11.7 1.8 broadcast_select_fusion
  13.6 2.7 gather_fusion.3
  16.3 78.1 %all_to_all.20 = bf16[96,128,128]{2,1,0:T(8,128)(2,1)} all-to-all(bf16[96,128,128]{2,1,0:T(8,128)(2,1)} %gather_fusion.3), channel_id=1, replica_groups=mesh['dom'=8,'dir'=4] {'dom'}, dimensions={0} | all-to-all | bytes 6291456 | tf_op jit(solution)/shard_map/all_to_all | solution.py:203
  94.4 1.0 copy-done.4
  95.4 4.3 gather_fusion
  99.8 3.6 all-to-all-start
  119.6 2.5 fusion.102
  126.0 1.5 neg.16
  127.5 1.8 copy.37
  129.3 1.3 gather_fusion.2
  130.6 3.3 copy.39
  134.7 6.1 %all-to-all-start.2 = ((bf16[96,4,128]{2,1,0:T(4,128)(2,1)}), bf16[96,4,128]{2,1,0:T(4,128)(2,1)S(1)}, u32[]{:S(2)}, u32[]{:S(2)}) async-start(bf16[96,4,128]{2,1,0:T(4,128)(2,1)} %gather_fusion.2), calls=%async_computation.2 | async-start | bytes 196608 | tf_op jit(solution)/shard_map/all_to_all | solution.py:204
  141.0 18.1 %gather_fusion.1 = bf16[6144,128]{1,0:T(8,128)(2,1)S(1)} fusion(bf16[3072,128]{1,0:T(8,128)(2,1)S(1)} %pad_maximum_fusion.3, s32[6144]{0:T(1024)S(1)} %broadcast_clamp_fusion), kind=kCustom, calls=%fused_computation.1 | custom fusion | bytes 3170304 | tf_op jit(solution)/shard_map/gather | solution.py:108
  159.2 1.2 fusion.48
  160.6 1.2 fusion.55
  161.9 1.2 fusion.62
  163.2 1.2 fusion.69
  164.4 1.2 fusion.76
  165.8 1.2 fusion.83
  167.0 1.6 copy-done.13
  168.6 33.9 %scatter_custom_fusion = f32[3072,128]{1,0:T(8,128)S(1)} fusion(s32[6144]{0:T(1024)} %reshape.1056, f32[6144,128]{1,0:T(8,128)} %bitcast.296, f32[]{:T(128)} %constant.151.clone.1), kind=kCustom, calls=%fused_computation.118 | custom fusion | flops 786432 | bytes 1573376 | tf_op jit(solution)/shard_map/scatter-add | solution.py:117
  202.5 0.9 slice.596
  203.5 6.0 %all-to-all-start.1 = ((f32[32,32,128]{2,1,0:T(8,128)}), f32[32,32,128]{2,1,0:T(8,128)S(1)}, u32[]{:S(2)}, u32[]{:S(2)}) async-start(f32[32,32,128]{2,1,0:T(8,128)} %bitcast.52), calls=%async_computation.1 | async-start | bytes 1048576 | tf_op jit(solution)/shard_map/all_to_all | solution.py:121
  209.9 0.9 slice_bitcast_fusion.8
  210.8 9.3 %all_gather.6 = bf16[384,4,128]{2,1,0:T(4,128)(2,1)S(1)} all-gather(bf16[96,4,128]{2,1,0:T(4,128)(2,1)S(1)} %all-to-all-done.2), channel_id=1, replica_groups=mesh['dom'=8,'dir'=4] {'dir'}, dimensions={0}, use_global_device_ids=true | all-gather | bytes 491520 | tf_op jit(solution)/shard_map/all_gather | solution.py:208
  220.2 6.9 %fusion.84 = s32[384]{0:T(512)S(1)} fusion(bf16[384,4,128]{2,1,0:T(4,128)(2,1)S(1)} %all_gather.6), kind=kLoop, calls=%fused_computation.178 | loop fusion | flops 384 | bytes 2304 | tf_op jit(solution)/shard_map/convert_element_type | solution.py:141
  227.9 7.4 %scatter_custom_fusion.1 = f32[2049,128]{1,0:T(8,128)S(1)} fusion(s32[1024]{0:T(1024)} %reshape.1064, f32[1024,128]{1,0:T(8,128)} %bitcast.295, f32[]{:T(128)} %constant.151.clone.1), kind=kCustom, calls=%fused_computation.120 | custom fusion | flops 131072 | bytes 1049600 | tf_op jit(solution)/shard_map/scatter-add | solution.py:128
  235.3 2.3 slice_add_fusion
  237.6 183.9 %while.13 = (s32[]{:T(128)}, f32[16,4,64,128]{3,0,2,1:T(8,128)S(1)}, f32[16,4,64,128]{3,0,2,1:T(8,128)}, s32[3,128]{1,0:T(4,128)S(1)}, bf16[3,128,3,128]{3,1,2,0...) while((s32[]{:T(128)}, ...), condition=%wide.region_6.7_spmd.clone, body=%wide.region_5.6_spmd.clone.sunk | while | flops 2447904768 | bytes 113871504 | solution.py:172
  260.8 2.6 multiply_divide_fusion.15
  267.2 2.6 multiply_divide_fusion.16
  269.8 2.1 fusion.150
  271.9 2.6 multiply_divide_fusion.17
  275.3 1.4 broadcast_multiply_fusion.9
  276.7 2.0 copy-done
  278.7 6.9 %fusion.151 = bf16[128,4,64,128]{3,2,1,0:T(8,128)(2,1)} fusion(f32[128,4,128]{2,1,0:T(4,128)S(1)} %get-tuple-element.266, f32[128,64,128]{2,1,0:T(8,128)S(1)} %bitcast.288, bf16[3,128,128,128]{3,2,1,0:T(8,128)(2,1)} %get-tuple-element.306, s32[]{:T(128)S(6)} %copy.78), kind=kOutput, calls=%fused_computation.20.clone.1 | convolution fusion | flops 1086324736 | bytes 17039364 | tf_op jit(solution)/shard_map/while/body/eval_jaxpr/gcqb,gbn->gcqn/dot_general | solution.py:151
  285.7 8.2 %select_add_fusion.4 = f32[16,4,64,128]{3,0,2,1:T(8,128)S(1)} fusion(f32[16,4,64,128]{3,0,2,1:T(8,128)S(1)} %get-tuple-element.292, bf16[128,4,64,128]{3,2,1,0:T(8,128)(2,1)} %fusion.151, pred[]{:T(512)S(6)} %compare.55, s32[128]{0:T(128)S(1)} %fusion.152), kind=kOutput, calls=%fused_computation.26.clone.1 | convolution fusion | flops 135268352 | bytes 12583425 | tf_op jit(solution)/shard_map/while/body/eval_jaxpr/lg,gcqn->lcqn/dot_general | solution.py:158
  294.4 4.8 %fusion.153 = bf16[128,4,64,128]{3,2,1,0:T(8,128)(2,1)S(1)} fusion(f32[128,4,128]{2,1,0:T(4,128)S(1)} %get-tuple-element.281, f32[128,64,128]{2,1,0:T(8,128)S(1)} %neg.19, bf16[3,128,128,128]{3,2,1,0:T(8,128)(2,1)} %get-tuple-element.306, s32[]{:T(128)S(6)} %copy.78), kind=kOutput, calls=%fused_computation.19.clone.1 | convolution fusion | flops 1086324736 | bytes 17039364 | tf_op jit(solution)/shard_map/while/body/eval_jaxpr/gcqb,gbn->gcqn/dot_general | solution.py:154
  299.2 6.0 %select_add_fusion.5 = f32[16,4,64,128]{3,0,2,1:T(8,128)} fusion(f32[16,4,64,128]{3,0,2,1:T(8,128)} %get-tuple-element.293, bf16[128,4,64,128]{3,2,1,0:T(8,128)(2,1)S(1)} %fusion.153, pred[]{:T(512)S(6)} %compare.55, s32[128]{0:T(128)S(1)} %fusion.152), kind=kOutput, calls=%fused_computation.25.clone.1 | convolution fusion | flops 135268352 | bytes 12583425 | tf_op jit(solution)/shard_map/while/body/eval_jaxpr/lg,gcqn->lcqn/dot_general | solution.py:161
  317.2 2.6 multiply_divide_fusion.15
  323.7 2.6 multiply_divide_fusion.16
  326.3 2.1 fusion.150
  328.3 2.6 multiply_divide_fusion.17
  331.8 1.4 broadcast_multiply_fusion.9
  333.2 2.0 copy-done
  335.2 6.9 %fusion.151 = bf16[128,4,64,128]{3,2,1,0:T(8,128)(2,1)} fusion(f32[128,4,128]{2,1,0:T(4,128)S(1)} %get-tuple-element.266, f32[128,64,128]{2,1,0:T(8,128)S(1)} %bitcast.288, bf16[3,128,128,128]{3,2,1,0:T(8,128)(2,1)} %get-tuple-element.306, s32[]{:T(128)S(6)} %copy.78), kind=kOutput, calls=%fused_computation.20.clone.1 | convolution fusion | flops 1086324736 | bytes 17039364 | tf_op jit(solution)/shard_map/while/body/eval_jaxpr/gcqb,gbn->gcqn/dot_general | solution.py:151
  342.1 8.2 %select_add_fusion.4 = f32[16,4,64,128]{3,0,2,1:T(8,128)S(1)} fusion(f32[16,4,64,128]{3,0,2,1:T(8,128)S(1)} %get-tuple-element.292, bf16[128,4,64,128]{3,2,1,0:T(8,128)(2,1)} %fusion.151, pred[]{:T(512)S(6)} %compare.55, s32[128]{0:T(128)S(1)} %fusion.152), kind=kOutput, calls=%fused_computation.26.clone.1 | convolution fusion | flops 135268352 | bytes 12583425 | tf_op jit(solution)/shard_map/while/body/eval_jaxpr/lg,gcqn->lcqn/dot_general | solution.py:158
  350.8 4.8 %fusion.153 = bf16[128,4,64,128]{3,2,1,0:T(8,128)(2,1)S(1)} fusion(f32[128,4,128]{2,1,0:T(4,128)S(1)} %get-tuple-element.281, f32[128,64,128]{2,1,0:T(8,128)S(1)} %neg.19, bf16[3,128,128,128]{3,2,1,0:T(8,128)(2,1)} %get-tuple-element.306, s32[]{:T(128)S(6)} %copy.78), kind=kOutput, calls=%fused_computation.19.clone.1 | convolution fusion | flops 1086324736 | bytes 17039364 | tf_op jit(solution)/shard_map/while/body/eval_jaxpr/gcqb,gbn->gcqn/dot_general | solution.py:154
  355.6 7.6 %select_add_fusion.5 = f32[16,4,64,128]{3,0,2,1:T(8,128)} fusion(f32[16,4,64,128]{3,0,2,1:T(8,128)} %get-tuple-element.293, bf16[128,4,64,128]{3,2,1,0:T(8,128)(2,1)S(1)} %fusion.153, pred[]{:T(512)S(6)} %compare.55, s32[128]{0:T(128)S(1)} %fusion.152), kind=kOutput, calls=%fused_computation.25.clone.1 | convolution fusion | flops 135268352 | bytes 12583425 | tf_op jit(solution)/shard_map/while/body/eval_jaxpr/lg,gcqn->lcqn/dot_general | solution.py:161
  375.3 2.6 multiply_divide_fusion.15
  381.7 2.6 multiply_divide_fusion.16
  384.3 2.1 fusion.150
  386.4 2.6 multiply_divide_fusion.17
  389.8 1.4 broadcast_multiply_fusion.9
  391.2 2.0 copy-done
  393.2 6.9 %fusion.151 = bf16[128,4,64,128]{3,2,1,0:T(8,128)(2,1)} fusion(f32[128,4,128]{2,1,0:T(4,128)S(1)} %get-tuple-element.266, f32[128,64,128]{2,1,0:T(8,128)S(1)} %bitcast.288, bf16[3,128,128,128]{3,2,1,0:T(8,128)(2,1)} %get-tuple-element.306, s32[]{:T(128)S(6)} %copy.78), kind=kOutput, calls=%fused_computation.20.clone.1 | convolution fusion | flops 1086324736 | bytes 17039364 | tf_op jit(solution)/shard_map/while/body/eval_jaxpr/gcqb,gbn->gcqn/dot_general | solution.py:151
  400.2 8.2 %select_add_fusion.4 = f32[16,4,64,128]{3,0,2,1:T(8,128)S(1)} fusion(f32[16,4,64,128]{3,0,2,1:T(8,128)S(1)} %get-tuple-element.292, bf16[128,4,64,128]{3,2,1,0:T(8,128)(2,1)} %fusion.151, pred[]{:T(512)S(6)} %compare.55, s32[128]{0:T(128)S(1)} %fusion.152), kind=kOutput, calls=%fused_computation.26.clone.1 | convolution fusion | flops 135268352 | bytes 12583425 | tf_op jit(solution)/shard_map/while/body/eval_jaxpr/lg,gcqn->lcqn/dot_general | solution.py:158
  408.9 4.8 %fusion.153 = bf16[128,4,64,128]{3,2,1,0:T(8,128)(2,1)S(1)} fusion(f32[128,4,128]{2,1,0:T(4,128)S(1)} %get-tuple-element.281, f32[128,64,128]{2,1,0:T(8,128)S(1)} %neg.19, bf16[3,128,128,128]{3,2,1,0:T(8,128)(2,1)} %get-tuple-element.306, s32[]{:T(128)S(6)} %copy.78), kind=kOutput, calls=%fused_computation.19.clone.1 | convolution fusion | flops 1086324736 | bytes 17039364 | tf_op jit(solution)/shard_map/while/body/eval_jaxpr/gcqb,gbn->gcqn/dot_general | solution.py:154
  413.7 7.6 %select_add_fusion.5 = f32[16,4,64,128]{3,0,2,1:T(8,128)} fusion(f32[16,4,64,128]{3,0,2,1:T(8,128)} %get-tuple-element.293, bf16[128,4,64,128]{3,2,1,0:T(8,128)(2,1)S(1)} %fusion.153, pred[]{:T(512)S(6)} %compare.55, s32[128]{0:T(128)S(1)} %fusion.152), kind=kOutput, calls=%fused_computation.25.clone.1 | convolution fusion | flops 135268352 | bytes 12583425 | tf_op jit(solution)/shard_map/while/body/eval_jaxpr/lg,gcqn->lcqn/dot_general | solution.py:161
  421.5 2.1 fusion.35
  423.7 3.8 convolution_bitcast_fusion
  427.5 3.8 convolution_bitcast_fusion.2
  431.4 3.8 fusion.33
  435.2 4.1 fusion.31
  (210 shorter events, 18.7 us)
Async XLA Ops:
  7.2 230.4 %all-gather.2.cloned.1.call-start = ((), (), s32[]{:S(2)}) async-start(), calls=%async_computation.4 | async-start | bytes 15728640 | tf_op jit(solution)/shard_map/all_gather | solution.py:207
  94.4 24.9 %copy-start.12 = (s32[6,1024]{1,0:T(8,128)S(1)}, s32[6,1024]{1,0:T(8,128)}, u32[]{:S(2)}) copy-start(s32[6,1024]{1,0:T(8,128)} %param.15) | copy-start | bytes 73732
  94.4 25.0 %copy-start.57 = (s32[32]{0:T(128)S(1)}, s32[32]{0:T(128)}, u32[]{:S(2)}) copy-start(s32[32]{0:T(128)} %param.22) | copy-start | bytes 388
  94.4 25.0 %copy-start.16 = (bf16[32,3,128]{2,0,1:T(8,128)(2,1)S(1)}, bf16[32,3,128]{2,0,1:T(8,128)(2,1)}, u32[]{:S(2)}) copy-start(bf16[32,3,128]{2,0,1:T(8,128)(2,1)} %param.19) | copy-start | bytes 73732
  94.4 28.5 %copy-start.15 = (f32[3,4]{1,0:T(4,128)S(1)}, f32[3,4]{1,0:T(4,128)}, u32[]{:S(2)}) copy-start(f32[3,4]{1,0:T(4,128)} %param.23) | copy-start | bytes 148
  94.4 29.1 %copy-start.11 = (f32[36,1024]{1,0:T(8,128)S(1)}, f32[36,1024]{1,0:T(8,128)}, u32[]{:S(2)}) copy-start(f32[36,1024]{1,0:T(8,128)} %param.16) | copy-start | bytes 442372
  95.4 29.2 %copy-start.14 = (s32[32,32]{1,0:T(8,128)S(1)}, s32[32,32]{1,0:T(8,128)}, u32[]{:S(2)}) copy-start(s32[32,32]{1,0:T(8,128)} %param.14) | copy-start | bytes 12292
  99.8 35.0 %all-to-all-start = ((bf16[32,32,128]{2,1,0:T(8,128)(2,1)}), bf16[32,32,128]{2,1,0:T(8,128)(2,1)S(1)}, u32[]{:S(2)}, u32[]{:S(2)}) async-start(bf16[32,32,128]{2,1,0:T(8,128)(2,1)} %bitcast.2), calls=%async_computation | async-start | bytes 524288 | tf_op jit(solution)/shard_map/all_to_all | solution.py:106
  119.6 7.9 %copy-start.49 = (f32[3,64]{1,0:T(4,128)}, f32[3,64]{1,0:T(4,128)S(1)}, u32[]{:S(2)}) copy-start(f32[3,64]{1,0:T(4,128)S(1)} %get-tuple-element.176) | copy-start | bytes 2308
  134.7 68.7 %all-to-all-start.2 = ((bf16[96,4,128]{2,1,0:T(4,128)(2,1)}), bf16[96,4,128]{2,1,0:T(4,128)(2,1)S(1)}, u32[]{:S(2)}, u32[]{:S(2)}) async-start(bf16[96,4,128]{2,1,0:T(4,128)(2,1)} %gather_fusion.2), calls=%async_computation.2 | async-start | bytes 196608 | tf_op jit(solution)/shard_map/all_to_all | solution.py:204
  140.9 18.3 %copy-start.24 = (f32[1,1024]{1,0:T(1,128)S(1)}, f32[1,1024]{1,0:T(1,128)}, u32[]{:S(2)}) copy-start(f32[1,1024]{1,0:T(1,128)} %get-tuple-element.153) | copy-start | bytes 12292
  140.9 18.3 %copy-start.25 = (f32[1,1024]{1,0:T(1,128)S(1)}, f32[1,1024]{1,0:T(1,128)}, u32[]{:S(2)}) copy-start(f32[1,1024]{1,0:T(1,128)} %get-tuple-element.154) | copy-start | bytes 12292
  140.9 18.3 %copy-start.26 = (f32[1,1024]{1,0:T(1,128)S(1)}, f32[1,1024]{1,0:T(1,128)}, u32[]{:S(2)}) copy-start(f32[1,1024]{1,0:T(1,128)} %get-tuple-element.155) | copy-start | bytes 12292
  140.9 18.3 %copy-start.27 = (f32[1,1024]{1,0:T(1,128)S(1)}, f32[1,1024]{1,0:T(1,128)}, u32[]{:S(2)}) copy-start(f32[1,1024]{1,0:T(1,128)} %get-tuple-element.156) | copy-start | bytes 12292
  140.9 18.3 %copy-start.28 = (f32[1,1024]{1,0:T(1,128)S(1)}, f32[1,1024]{1,0:T(1,128)}, u32[]{:S(2)}) copy-start(f32[1,1024]{1,0:T(1,128)} %get-tuple-element.157) | copy-start | bytes 12292
  140.9 18.3 %copy-start.29 = (f32[1,1024]{1,0:T(1,128)S(1)}, f32[1,1024]{1,0:T(1,128)}, u32[]{:S(2)}) copy-start(f32[1,1024]{1,0:T(1,128)} %get-tuple-element.158) | copy-start | bytes 12292
  140.9 19.5 %copy-start.18 = (f32[1,1024]{1,0:T(1,128)S(1)}, f32[1,1024]{1,0:T(1,128)}, u32[]{:S(2)}) copy-start(f32[1,1024]{1,0:T(1,128)} %get-tuple-element.147) | copy-start | bytes 12292
  140.9 19.5 %copy-start.19 = (f32[1,1024]{1,0:T(1,128)S(1)}, f32[1,1024]{1,0:T(1,128)}, u32[]{:S(2)}) copy-start(f32[1,1024]{1,0:T(1,128)} %get-tuple-element.148) | copy-start | bytes 12292
  140.9 19.5 %copy-start.20 = (f32[1,1024]{1,0:T(1,128)S(1)}, f32[1,1024]{1,0:T(1,128)}, u32[]{:S(2)}) copy-start(f32[1,1024]{1,0:T(1,128)} %get-tuple-element.149) | copy-start | bytes 12292
  140.9 19.5 %copy-start.21 = (f32[1,1024]{1,0:T(1,128)S(1)}, f32[1,1024]{1,0:T(1,128)}, u32[]{:S(2)}) copy-start(f32[1,1024]{1,0:T(1,128)} %get-tuple-element.150) | copy-start | bytes 12292
  141.0 19.5 %copy-start.22 = (f32[1,1024]{1,0:T(1,128)S(1)}, f32[1,1024]{1,0:T(1,128)}, u32[]{:S(2)}) copy-start(f32[1,1024]{1,0:T(1,128)} %get-tuple-element.151) | copy-start | bytes 12292
  141.0 19.5 %copy-start.23 = (f32[1,1024]{1,0:T(1,128)S(1)}, f32[1,1024]{1,0:T(1,128)}, u32[]{:S(2)}) copy-start(f32[1,1024]{1,0:T(1,128)} %get-tuple-element.152) | copy-start | bytes 12292
  159.1 2.7 copy-start.17
  159.1 2.7 copy-start.46
  159.1 2.7 copy-start.47
  159.1 2.7 copy-start.48
  159.2 3.9 copy-start.40
  159.2 3.9 copy-start.41
  159.2 3.9 copy-start.42
  159.2 3.9 copy-start.43
  159.2 3.9 copy-start.44
  159.2 3.9 copy-start.45
  160.5 3.9 copy-start.34
  160.5 3.9 copy-start.35
  160.5 3.9 copy-start.36
  160.6 3.9 copy-start.37
  160.6 3.9 copy-start.38
  160.6 3.9 copy-start.39
  161.8 3.9 copy-start.30
  161.9 3.9 copy-start.31
  161.9 3.9 copy-start.32
  161.9 3.9 copy-start.33
  165.7 43.8 %copy-start.51 = (f32[4]{0:T(128)S(1)}, f32[4]{0:T(128)}, u32[]{:S(2)}) copy-start(f32[4]{0:T(128)} %get-tuple-element.169) | copy-start | bytes 52
  165.7 43.8 %copy-start.52 = (f32[4]{0:T(128)S(1)}, f32[4]{0:T(128)}, u32[]{:S(2)}) copy-start(f32[4]{0:T(128)} %get-tuple-element.170) | copy-start | bytes 52
  165.7 43.8 %copy-start.53 = (f32[4]{0:T(128)S(1)}, f32[4]{0:T(128)}, u32[]{:S(2)}) copy-start(f32[4]{0:T(128)} %get-tuple-element.171) | copy-start | bytes 52
  165.7 43.8 %copy-start.54 = (f32[64]{0:T(128)S(1)}, f32[64]{0:T(128)}, u32[]{:S(2)}) copy-start(f32[64]{0:T(128)} %get-tuple-element.172) | copy-start | bytes 772
  165.7 43.8 %copy-start.55 = (f32[64]{0:T(128)S(1)}, f32[64]{0:T(128)}, u32[]{:S(2)}) copy-start(f32[64]{0:T(128)} %get-tuple-element.173) | copy-start | bytes 772
  165.7 43.8 %copy-start.56 = (f32[64]{0:T(128)S(1)}, f32[64]{0:T(128)}, u32[]{:S(2)}) copy-start(f32[64]{0:T(128)} %get-tuple-element.174) | copy-start | bytes 772
  165.7 43.9 %copy-start.50 = (f32[3,64]{1,0:T(4,128)S(1)}, f32[3,64]{1,0:T(4,128)}, u32[]{:S(2)}) copy-start(f32[3,64]{1,0:T(4,128)} %copy-done.49) | copy-start | bytes 2308
  167.0 1.6 copy-start.13
  202.5 7.4 %copy-start.3 = (f32[3072,128]{1,0:T(8,128)}, f32[3072,128]{1,0:T(8,128)S(1)}, u32[]{:S(2)}) copy-start(f32[3072,128]{1,0:T(8,128)S(1)} %scatter_custom_fusion) | copy-start | bytes 4718596
  203.5 23.6 %all-to-all-start.1 = ((f32[32,32,128]{2,1,0:T(8,128)}), f32[32,32,128]{2,1,0:T(8,128)S(1)}, u32[]{:S(2)}, u32[]{:S(2)}) async-start(f32[32,32,128]{2,1,0:T(8,128)} %bitcast.52), calls=%async_computation.1 | async-start | bytes 1048576 | tf_op jit(solution)/shard_map/all_to_all | solution.py:121
  210.8 26.7 %copy-start.2 = (f32[16,4,64,128]{3,0,2,1:T(8,128)S(1)}, f32[16,4,64,128]{3,0,2,1:T(8,128)}, u32[]{:S(2)}) copy-start(f32[16,4,64,128]{3,0,2,1:T(8,128)} %custom-call) | copy-start | bytes 6291460
  276.7 2.0 copy-start
  285.7 8.2 %copy-start.1 = (f32[128,4,4,4,128]{4,3,2,1,0:T(4,128)S(1)}, f32[128,4,4,4,128]{4,3,2,1,0:T(4,128)}, u32[]{:S(2)}) copy-start(f32[128,4,4,4,128]{4,3,2,1,0:T(4,128)} %copy-done) | copy-start | bytes 12582916 | tf_op jit(solution)/shard_map/while
  333.2 2.0 copy-start
  342.1 8.2 %copy-start.1 = (f32[128,4,4,4,128]{4,3,2,1,0:T(4,128)S(1)}, f32[128,4,4,4,128]{4,3,2,1,0:T(4,128)}, u32[]{:S(2)}) copy-start(f32[128,4,4,4,128]{4,3,2,1,0:T(4,128)} %copy-done) | copy-start | bytes 12582916 | tf_op jit(solution)/shard_map/while
  391.2 2.0 copy-start
  400.2 8.2 %copy-start.1 = (f32[128,4,4,4,128]{4,3,2,1,0:T(4,128)S(1)}, f32[128,4,4,4,128]{4,3,2,1,0:T(4,128)}, u32[]{:S(2)}) copy-start(f32[128,4,4,4,128]{4,3,2,1,0:T(4,128)} %copy-done) | copy-start | bytes 12582916 | tf_op jit(solution)/shard_map/while
  421.5 2.2 copy-start.7
  421.5 2.2 copy-start.8
  421.5 2.2 copy-start.9
  421.5 2.2 copy-start.10
  423.6 7.7 %copy-start.6 = (f32[8,64,64]{1,0,2:T(8,128)S(1)}, f32[8,64,64]{1,0,2:T(8,128)}, u32[]{:S(2)}) copy-start(f32[8,64,64]{1,0,2:T(8,128)} %copy.37) | copy-start | bytes 393220
  (2 other events, 1.8 us)
Sparse Core Ops, SparseCore 0:
  94.5 83.8 all-gather.1
where the time goes:
time: 454 us; the launch traced here: 447 us
  other arithmetic  107 us (24%)
  matrix products  96.7 us (21%)
  blocking collectives  87.4 us (19%)
  loops' own time  57 us (13%)
  local copies, waits for them, and re-layouts  53 us (12%)
  between operations  30.8 us (7%)
  starting transfers between devices  15.7 us (3%)
    all_to_all x1, blocking collectives, boundary_part(): lax.all_to_all(packed_blocks, 'dom', split_axis=0, concat_axis=0, tiled=T...  78.1 us
    another operation x1, loops' own time, expand_leaves(): sums, unused = lax.scan(one_group, (empty, empty), inputs)  57 us
    scatter-add x1, other arithmetic, interior_part(): jax.ops.segment_sum(stacked, connectivity.reshape(-1), num_segments=owned...  33.9 us
    div x10, other arithmetic, lagrange(): product * (points - node_values[other_node])  25.7 us
    dot_general x3, matrix products, one_group(): jnp.einsum('lg,gcqn->lcqn', selector, real_part, preferred_element_type=j...  24.6 us
    dot_general x3, matrix products, one_group(): jnp.einsum('lg,gcqn->lcqn', selector, imag_part, preferred_element_type=j...  21.3 us
    dot_general x3, matrix products, one_group(): jnp.einsum('gcqb,gbn->gcqn', real_w, blocks_now, preferred_element_type=j...  20.8 us
    gather x1, local copies, waits for them, and re-layouts, interior_part(): gathered = edge_table[connectivity]  18.1 us
  transfers between devices with their start and end apart: 4, of which 0 were waited for; matrix products, arithmetic and copies ran while one was open for 22% of the time, Pallas kernels for 0%

commit v1 on v0

--- a/solution.py
+++ b/solution.py
@@ -1,6 +1,8 @@
 import jax
 import jax.numpy as jnp
 from jax import lax
+from jax.experimental import pallas as pl
+from jax.experimental.pallas import tpu as pltpu
 from jax.sharding import PartitionSpec as P
 
 LEAVES_DEV = 16
@@ -131,46 +133,73 @@
     return assembled[:owned_rows] + folded[:owned_rows]
 
 
+def block_sums(leaf_ids, factors, blocks, cone_count):
+    block_count, block_size, columns = blocks.shape
+    rows = factors.shape[1]
+    plane = NODES * NODES
+    height = 2 * cone_count * NODES**3
+    group = next(size for size in (8, 4, 2, 1) if block_count % size == 0)
+
+    def kernel(leaf_ref, factor_ref, block_ref, out_ref):
+        step = pl.program_id(0)
+
+        @pl.when(step == 0)
+        def _():
+            out_ref[...] = jnp.zeros_like(out_ref)
+
+        for g in range(group):
+            pairs = factor_ref[g, :plane, :]
+            first = factor_ref[g, plane : plane + NODES, :]
+            pieces = []
+            for wave in range(2 * cone_count):
+                at = plane + NODES + wave
+                scaled = first * factor_ref[g, at : at + 1, :]
+                for digit in range(NODES):
+                    pieces.append((scaled[digit : digit + 1] * pairs).astype(jnp.bfloat16))
+            weights = jnp.concatenate(pieces, axis=0)
+            product = jnp.dot(weights, block_ref[g], preferred_element_type=jnp.float32)
+            leaf = leaf_ref[step * group + g]
+            out_ref[leaf] += product
+
+    return pl.pallas_call(
+        kernel,
+        out_shape=jax.ShapeDtypeStruct((LEAVES_DEV, height, columns), jnp.float32),
+        grid_spec=pltpu.PrefetchScalarGridSpec(
+            num_scalar_prefetch=1,
+            grid=(block_count // group,),
+            in_specs=[
+                pl.BlockSpec((group, rows, block_size), lambda i, leaf: (i, 0, 0)),
+                pl.BlockSpec((group, block_size, columns), lambda i, leaf: (i, 0, 0)),
+            ],
+            out_specs=pl.BlockSpec((LEAVES_DEV, height, columns), lambda i, leaf: (0, 0, 0)),
+        ),
+        cost_estimate=pl.CostEstimate(
+            flops=2 * block_count * height * block_size * columns,
+            bytes_accessed=block_count * block_size * (rows * 4 + columns * 2),
+            transcendentals=0,
+        ),
+    )(leaf_ids, factors, blocks)
+
+
 def expand_leaves(arrived_blocks, arrived_meta, waves):
-    block_size = arrived_blocks.shape[1]
     columns = arrived_blocks.shape[2]
     cone_count = waves.shape[1]
     square = NODES**3
-    group_rows = 512 // cone_count
-    group_count = arrived_blocks.shape[0] // group_rows
     leaf_ids = arrived_meta[:, 3, 0].astype(jnp.int32)
-
-    def one_group(carry, inputs):
-        real_sum, imag_sum = carry
-        blocks_now, coords, leaves = inputs
-        coords_wide = coords.astype(jnp.float32)
-        basis_now = tensor_basis(coords_wide)
-        phase_now = wave_phase(waves, coords_wide)
-        real_w = (basis_now[:, None] * jnp.cos(phase_now)[:, :, None, :]).astype(jnp.bfloat16)
-        imag_w = (-basis_now[:, None] * jnp.sin(phase_now)[:, :, None, :]).astype(jnp.bfloat16)
-        real_part = jnp.einsum(
-            "gcqb,gbn->gcqn", real_w, blocks_now, preferred_element_type=jnp.float32
-        ).astype(jnp.bfloat16)
-        imag_part = jnp.einsum(
-            "gcqb,gbn->gcqn", imag_w, blocks_now, preferred_element_type=jnp.float32
-        ).astype(jnp.bfloat16)
-        selector = (jnp.arange(LEAVES_DEV)[:, None] == leaves[None, :]).astype(jnp.bfloat16)
-        real_sum = real_sum + jnp.einsum(
-            "lg,gcqn->lcqn", selector, real_part, preferred_element_type=jnp.float32
-        )
-        imag_sum = imag_sum + jnp.einsum(
-            "lg,gcqn->lcqn", selector, imag_part, preferred_element_type=jnp.float32
-        )
-        return ((real_sum, imag_sum), None)
-
-    empty = jnp.zeros((LEAVES_DEV, cone_count, square, columns), jnp.float32)
-    inputs = (
-        arrived_blocks.reshape(group_count, group_rows, block_size, columns),
-        arrived_meta[:, :3].reshape(group_count, group_rows, 3, block_size),
-        leaf_ids.reshape(group_count, group_rows),
-    )
-    sums, unused = lax.scan(one_group, (empty, empty), inputs)
-    real_sum, imag_sum = sums
+    coords = arrived_meta[:, :3].astype(jnp.float32)
+    second = lagrange(coords[:, 1])
+    third = lagrange(coords[:, 2])
+    pairs = (second[:, :, None] * third[:, None, :]).reshape(
+        coords.shape[0], NODES * NODES, coords.shape[2]
+    )
+    phase = wave_phase(waves, coords)
+    factors = jnp.concatenate(
+        [pairs, lagrange(coords[:, 0]), jnp.cos(phase), -jnp.sin(phase)], axis=1
+    )
+    sums = block_sums(leaf_ids, factors, arrived_blocks, cone_count).reshape(
+        LEAVES_DEV, 2, cone_count, square, columns
+    )
+    real_sum, imag_sum = sums[:, 0], sums[:, 1]
     node_phase = wave_phase(waves, node_coords())
     cosine = jnp.cos(node_phase)[None, :, :, None]
     sine_part = jnp.sin(node_phase)[None, :, :, None]

time: 454 us -> 350 us (0.77)
  matrix products: 96.7 us -> 15.5 us
  loops' own time: 57 us -> 0 us
  Pallas kernels: 0 us -> 40.2 us
  other arithmetic: 107 us -> 94.6 us
  local copies, waits for them, and re-layouts: 53 us -> 58.7 us
    dot_general x12 -> x0, matrix products: 81.2 us -> none  [the longest x3 24.6 us: one_group(): jnp.einsum('lg,gcqn->lcqn', selector, real_part, preferred_element_type=j...]
    another operation x1 -> x0, loops' own time: 57 us -> none  [expand_leaves(): sums, unused = lax.scan(one_group, (empty, empty), inputs)]
    pallas_call x0 -> x1, Pallas kernels: none -> 40.2 us  [block_sums(): pl.pallas_call(kernel, out_shape=jax.ShapeDtypeStruct((LEAVES_DEV, height...]
    concatenate x0 -> x1, local copies, waits for them, and re-layouts: none -> 14.5 us  [expand_leaves(): jnp.concatenate([pairs, lagrange(coords[:, 0]), jnp.cos(phase), -jnp.sin(...]
    div x10 -> x4, other arithmetic: 25.7 us -> 15.6 us  [lagrange(): product * (points - node_values[other_node])]
    sin x3 -> x0, other arithmetic: 6.21 us -> none  [one_group(): jnp.sin(phase_now)[:, :, None, :]]
    while x12 -> x0, local copies, waits for them, and re-layouts: 6.07 us -> none
    neg x3 -> x1, other arithmetic: 1.33 us -> 6.94 us  [expand_leaves(): -jnp.sin(phase)]
  transfers between devices with their start and end apart: 4 -> 4, of which waited for: 0 -> 0; matrix products, arithmetic and copies ran while one was open for 22% -> 40% of each run, Pallas kernels for 0% -> 0%
where the time goes in v1:
time: 350 us; the launch traced here: 344 us
  other arithmetic  94.6 us (27%)
  blocking collectives  89.5 us (26%)
  local copies, waits for them, and re-layouts  58.7 us (17%)
  Pallas kernels  40.2 us (11%)
  between operations  30.9 us (9%)
  matrix products  15.5 us (4%)
  starting transfers between devices  14.6 us (4%)
    all_to_all x1, blocking collectives, boundary_part(): lax.all_to_all(packed_blocks, 'dom', split_axis=0, concat_axis=0, tiled=T...  78.1 us
    pallas_call x1, Pallas kernels, block_sums(): pl.pallas_call(kernel, out_shape=jax.ShapeDtypeStruct((LEAVES_DEV, height...  40.2 us
    scatter-add x1, other arithmetic, interior_part(): jax.ops.segment_sum(stacked, connectivity.reshape(-1), num_segments=owned...  33.9 us
    gather x1, local copies, waits for them, and re-layouts, interior_part(): gathered = edge_table[connectivity]  18.1 us
    div x4, other arithmetic, lagrange(): product * (points - node_values[other_node])  15.6 us
    concatenate x1, local copies, waits for them, and re-layouts, expand_leaves(): jnp.concatenate([pairs, lagrange(coords[:, 0]), jnp.cos(phase), -jnp.sin(...  14.5 us
    all_gather x1, blocking collectives, boundary_part(): lax.all_gather(owner_meta, 'dir', axis=0, tiled=True)  11.4 us
    convert_element_type x1, other arithmetic, expand_leaves(): leaf_ids = arrived_meta[:, 3, 0].astype(jnp.int32)  7.48 us
  transfers between devices with their start and end apart: 4, of which 0 were waited for; matrix products, arithmetic and copies ran while one was open for 40% of the time, Pallas kernels for 0%

profile of v1, /device:TPU:0, one launch (start us, length us, event | category | flops | bytes accessed | tf_op | source)
XLA Modules:
  0.0 344.1 jit_solution(2901099271363651961)
XLA Ops:
  7.2 0.7 fusion.69
  8.0 0.8 select_reduce_fusion
  8.8 0.7 compare_select_fusion.3
  9.5 0.7 scatter_custom_fusion.2
  10.2 0.7 compare_select_fusion.1
  11.0 0.7 iota_compare_fusion.1
  11.7 1.8 broadcast_select_fusion
  13.5 0.1 concatenate.35
  13.6 2.7 gather_fusion.3
  16.3 78.1 %all_to_all.20 = bf16[96,128,128]{2,1,0:T(8,128)(2,1)} all-to-all(bf16[96,128,128]{2,1,0:T(8,128)(2,1)} %gather_fusion.3), channel_id=1, replica_groups=mesh['dom'=8,'dir'=4] {'dom'}, dimensions={0} | all-to-all | bytes 6291456 | tf_op jit(solution)/shard_map/all_to_all | solution.py:232
  94.4 0.7 copy-done.19
  95.1 0.1 broadcast_in_dim.86
  95.3 1.3 gather_fusion.2
  96.6 3.6 %all-to-all-start.2 = ((bf16[96,4,128]{2,1,0:T(4,128)(2,1)}), bf16[96,4,128]{2,1,0:T(4,128)(2,1)S(1)}, u32[]{:S(2)}, u32[]{:S(2)}) async-start(bf16[96,4,128]{2,1,0:T(4,128)(2,1)} %gather_fusion.2), calls=%async_computation.2 | async-start | bytes 196608 | tf_op jit(solution)/shard_map/all_to_all | solution.py:233
  100.3 0.7 fusion.108
  116.0 2.6 fusion.83
  118.6 0.5 broadcast_multiply_fusion.1
  119.1 1.5 neg.12
  120.6 1.3 copy.37
  122.0 0.7 reshape.1016
  122.6 2.9 copy.38
  126.2 4.3 %gather_fusion = bf16[1024,128]{1,0:T(8,128)(2,1)} fusion(bf16[2049,128]{1,0:T(8,128)(2,1)S(1)} %concatenate.30, s32[1024]{0:T(1024)S(1)} %get-tuple-element.92), kind=kCustom, calls=%fused_computation | custom fusion | bytes 528384 | tf_op jit(solution)/shard_map/gather | solution.py:107
  130.8 0.7 fusion.107
  131.5 0.7 fusion.106
  132.1 0.1 broadcast_subtract_fusion
  132.3 0.9 slice_bitcast_fusion.2
  133.2 0.7 fusion.96
  133.9 6.1 %all-to-all-start = ((bf16[32,32,128]{2,1,0:T(8,128)(2,1)}), bf16[32,32,128]{2,1,0:T(8,128)(2,1)S(1)}, u32[]{:S(2)}, u32[]{:S(2)}) async-start(bf16[32,32,128]{2,1,0:T(8,128)(2,1)} %bitcast.2), calls=%async_computation | async-start | bytes 524288 | tf_op jit(solution)/shard_map/all_to_all | solution.py:108
  140.0 11.4 %all_gather.6 = bf16[384,4,128]{2,1,0:T(4,128)(2,1)S(1)} all-gather(bf16[96,4,128]{2,1,0:T(4,128)(2,1)S(1)} %all-to-all-done.2), channel_id=1, replica_groups=mesh['dom'=8,'dir'=4] {'dir'}, dimensions={0}, use_global_device_ids=true | all-gather | bytes 491520 | tf_op jit(solution)/shard_map/all_gather | solution.py:237
  151.6 4.0 %fusion.63 = (f32[384,1,128]{2,1,0:T(1,128)}, f32[384,1,128]{2,1,0:T(1,128)}, f32[384,1,128]{2,1,0:T(1,128)}) fusion(f32[]{:T(128)S(6)} %sub.382, f32[]{:T(128)S(6)} %sub.381, f32[]{:T(128)S(6)} %sub.380, f32[]{:T(128)} %bitcast.63, f32[]{:T(128)} %bitcast.64, f32[]{:T(128)} %bitcast.62, f32[384,3,128]{2,1,0:T(4,128)S(1)} %slice_convert_fusion), kind=kLoop, calls=%fused_computation.161 | loop fusion | flops 1179648 | bytes 1179672 | tf_op jit(solution)/shard_map/div | solution.py:25
  155.5 0.7 sub.369
  156.2 4.9 %fusion.65 = (f32[384,1,128]{2,1,0:T(1,128)}, f32[384,1,128]{2,1,0:T(1,128)}, f32[384,1,128]{2,1,0:T(1,128)}, f32[384,1,128]{2,1,0:T(1,128)}, f32[384,1,128]{2,1,0:T(1,128)}, /*index=5*/f32[384,1,128]{2,1,0:T(1,128)}) fusion(f32[]{:T(128)S(6)} %sub.388, f32[]{:T(128)S(6)} %sub.387, f32[]{:T(128)S(6)} %sub.386, f32[]{:T(128)} %bitcast.63, f32[]{:T(128)} %bitcast.62, ...), kind=kLoop, calls=%fused_computation.163 | loop fusion | flops 2015232 | bytes 1966128 | tf_op jit(solution)/shard_map/div | solution.py:25
  161.2 4.1 %fusion.54 = (f32[384,1,128]{2,1,0:T(1,128)}, f32[384,1,128]{2,1,0:T(1,128)}, f32[384,1,128]{2,1,0:T(1,128)}, f32[384,1,128]{2,1,0:T(1,128)}, f32[384,1,128]{2,1,0:T(1,128)}, /*index=5*/f32[384,1,128]{2,1,0:T(1,128)}) fusion(f32[]{:T(128)S(6)} %sub.377, f32[]{:T(128)S(6)} %sub.374, f32[]{:T(128)S(6)} %sub.371, f32[]{:T(128)} %bitcast.63, f32[]{:T(128)} %bitcast.64, ...), kind=kLoop, calls=%fused_computation.152 | loop fusion | flops 1081344 | bytes 1966116 | tf_op jit(solution)/shard_map/div | solution.py:25
  165.4 18.1 %gather_fusion.1 = bf16[6144,128]{1,0:T(8,128)(2,1)S(1)} fusion(bf16[3072,128]{1,0:T(8,128)(2,1)S(1)} %pad_maximum_fusion, s32[6144]{0:T(1024)S(1)} %broadcast_clamp_fusion), kind=kCustom, calls=%fused_computation.1 | custom fusion | bytes 3170304 | tf_op jit(solution)/shard_map/gather | solution.py:110
  183.7 1.2 fusion.17
  185.0 1.2 fusion.24
  186.4 1.2 fusion.31
  187.6 1.2 fusion.38
  188.9 1.2 fusion.45
  190.1 1.2 fusion.52
  191.4 1.6 copy-done.17
  193.0 33.9 %scatter_custom_fusion = f32[3072,128]{1,0:T(8,128)S(1)} fusion(s32[6144]{0:T(1024)S(1)} %reshape.1008, f32[6144,128]{1,0:T(8,128)} %bitcast.228, f32[]{:T(128)} %constant.133.clone.1), kind=kCustom, calls=%fused_computation.65 | custom fusion | flops 786432 | bytes 1573376 | tf_op jit(solution)/shard_map/scatter-add | solution.py:119
  227.0 0.8 slice.580
  227.9 4.8 %all-to-all-start.1 = ((f32[32,32,128]{2,1,0:T(8,128)}), f32[32,32,128]{2,1,0:T(8,128)}, u32[]{:S(2)}, u32[]{:S(2)}) async-start(f32[32,32,128]{2,1,0:T(8,128)} %bitcast.52), calls=%async_computation.1 | async-start | bytes 1048576 | tf_op jit(solution)/shard_map/all_to_all | solution.py:123
  232.7 1.8 pad_maximum_fusion.2
  234.5 1.7 pad_maximum_fusion.1
  236.3 6.9 %sine_negate_fusion = (f32[384,4,128]{2,1,0:T(4,128)}, f32[384,4,128]{2,1,0:T(4,128)}) fusion(f32[384,128]{1,0:T(8,128)S(1)} %bitcast.227, f32[4]{0:T(128)S(1)} %copy-done.54, f32[384,128]{1,0:T(8,128)S(1)} %bitcast.226, f32[4]{0:T(128)S(1)} %copy-done.56, f32[384,128]{1,0:T(8,128)S(1)} %bitcast.225, f32[4]{0:T(128)S(1)} %copy-done.52), kind=kLoop, calls=%fused_computation.63 | loop fusion | flops 1179648 | bytes 2162736 | tf_op jit(solution)/shard_map/neg | solution.py:197
  243.2 0.8 broadcast_multiply_fusion
  244.0 14.5 %concatenate.34.factor_ref = f32[384,28,128]{2,1,0:T(8,128)} concatenate(f32[384,16,128]{2,1,0:T(8,128)S(1)} %bitcast.218, f32[384,1,128]{2,1,0:T(1,128)} %get-tuple-element.19, f32[384,1,128]{2,1,0:T(1,128)} %get-tuple-element.29, f32[384,1,128]{2,1,0:T(1,128)} %get-tuple-element.15, f32[384,1,128]{2,1,0:T(1,128)} %get-tuple-element.14, f32[384,4,128]{2,1,0:T(4,128)} %get-tuple-element.33, ...), dimensions={1} | concatenate | bytes 11010048 | tf_op jit(solution)/shard_map/concatenate | solution.py:196
  258.5 7.5 %fusion.53.leaf_ref = s32[384]{0:T(512)} fusion(bf16[384,4,128]{2,1,0:T(4,128)(2,1)S(1)} %all_gather.6), kind=kLoop, calls=%fused_computation.151 | loop fusion | flops 384 | bytes 2304 | tf_op jit(solution)/shard_map/convert_element_type | solution.py:188
  265.9 7.2 %scatter_custom_fusion.1 = f32[2049,128]{1,0:T(8,128)S(1)} fusion(s32[1024]{0:T(1024)} %reshape.1016, f32[1024,128]{1,0:T(8,128)} %bitcast.53, f32[]{:T(128)} %constant.133.clone.1), kind=kCustom, calls=%fused_computation.68 | custom fusion | flops 131072 | bytes 1049600 | tf_op jit(solution)/shard_map/scatter-add | solution.py:130
  273.2 2.3 slice_add_fusion
  275.5 40.2 %shard_map.122 = f32[16,512,128]{2,1,0:T(8,128)} custom-call(s32[384]{0:T(512)} %fusion.53.leaf_ref, f32[384,28,128]{2,1,0:T(8,128)} %concatenate.34.factor_ref, bf16[384,128,128]{2,1,0:T(8,128)(2,1)} %all-gather.2.cloned.1.call-done.block_ref), custom_call_target="tpu_custom_call" | custom-call | flops 6442450944 | bytes 18087936 | tf_op jit(solution)/shard_map/pallas_call | solution.py:164
  315.7 2.8 fusion.105
  318.5 0.2 copy.35
  318.7 0.2 copy.36
  319.0 0.4 copy-done.49
  319.4 0.7 add_convert_fusion
  320.1 0.2 copy-done.11
  320.6 3.9 %convolution_bitcast_fusion.2 = f32[4,2,128,64]{2,3,1,0:T(8,128)S(1)} fusion(bf16[2,8,4,64,128]{4,3,1,0,2:T(8,128)(2,1)S(1)} %get-tuple-element.10, f32[8,64,64]{2,1,0:T(8,128)S(1)} %copy-done.11, f32[8,64,64]{2,1,0:T(8,128)S(1)} %copy-done.13, f32[4]{0:T(128)S(1)} %copy-done.54, f32[8,64,64]{2,1,0:T(8,128)S(1)} %copy-done.14, f32[4]{0:T(128)S(1)} %copy-done.56, ...), kind=kOutput, calls=%fused_computation.48 | convolution fusion | flops 68157440 | bytes 1835056 | tf_op jit(solution)/shard_map/cops,xocsn->xcpn/dot_general | solution.py:213
  324.5 3.9 %convolution_bitcast_fusion = f32[4,2,128,64]{2,3,1,0:T(8,128)S(1)} fusion(bf16[2,8,4,64,128]{4,3,1,0,2:T(8,128)(2,1)S(1)} %get-tuple-element.11, f32[8,64,64]{2,1,0:T(8,128)S(1)} %copy-done.11, f32[8,64,64]{2,1,0:T(8,128)S(1)} %copy-done.13, f32[4]{0:T(128)S(1)} %copy-done.54, f32[8,64,64]{2,1,0:T(8,128)S(1)} %copy-done.14, f32[4]{0:T(128)S(1)} %copy-done.56, ...), kind=kOutput, calls=%fused_computation.46 | convolution fusion | flops 68157440 | bytes 1835056 | tf_op jit(solution)/shard_map/cops,xocsn->xcpn/dot_general | solution.py:216
  328.3 4.0 %fusion.1 = f32[2,4,1,64,128]{4,3,0,1,2:T(8,128)S(1)} fusion(f32[4,2,128,64]{2,3,1,0:T(8,128)S(1)} %convolution_bitcast_fusion.2, bf16[2,8,4,64,128]{4,3,1,0,2:T(8,128)(2,1)S(1)} %get-tuple-element.11, f32[8,64,64]{2,1,0:T(8,128)S(1)} %copy-done.13, f32[4]{0:T(128)S(1)} %copy-done.54, f32[8,64,64]{2,1,0:T(8,128)S(1)} %copy-done.14, f32[4]{0:T(128)S(1)} %copy-done.56, ...), kind=kOutput, calls=%fused_computation.51 | convolution fusion | flops 68222976 | bytes 2097200 | tf_op jit(solution)/shard_map/cops,xocsn->xcpn/dot_general | solution.py:211
  332.3 3.8 %fusion.3 = f32[2,4,1,64,128]{4,3,0,1,2:T(8,128)S(1)} fusion(f32[4,2,128,64]{2,3,1,0:T(8,128)S(1)} %convolution_bitcast_fusion, bf16[2,8,4,64,128]{4,3,1,0,2:T(8,128)(2,1)S(1)} %get-tuple-element.10, f32[8,64,64]{2,1,0:T(8,128)S(1)} %copy-done.13, f32[4]{0:T(128)S(1)} %copy-done.54, f32[8,64,64]{2,1,0:T(8,128)S(1)} %copy-done.14, f32[4]{0:T(128)S(1)} %copy-done.56, ...), kind=kOutput, calls=%fused_computation.53 | convolution fusion | flops 68222976 | bytes 2097200 | tf_op jit(solution)/shard_map/cops,xocsn->xcpn/dot_general | solution.py:214
  336.2 0.8 copy.39
  (151 shorter events, 1.3 us)
Async XLA Ops:
  7.2 268.3 %all-gather.2.cloned.1.call-start = ((), (), s32[]{:S(2)}) async-start(), calls=%async_computation.4 | async-start | bytes 15728640 | tf_op jit(solution)/shard_map/all_gather | solution.py:236
  94.4 0.7 copy-start.19
  94.4 0.8 copy-start.58
  96.6 37.3 %all-to-all-start.2 = ((bf16[96,4,128]{2,1,0:T(4,128)(2,1)}), bf16[96,4,128]{2,1,0:T(4,128)(2,1)S(1)}, u32[]{:S(2)}, u32[]{:S(2)}) async-start(bf16[96,4,128]{2,1,0:T(4,128)(2,1)} %gather_fusion.2), calls=%async_computation.2 | async-start | bytes 196608 | tf_op jit(solution)/shard_map/all_to_all | solution.py:233
  120.6 1.3 copy-start.18
  120.6 4.9 %copy-start.1 = (bf16[2048,128]{1,0:T(8,128)(2,1)S(1)}, bf16[2048,128]{1,0:T(8,128)(2,1)}, u32[]{:S(2)}) copy-start(bf16[2048,128]{1,0:T(8,128)(2,1)} %param.11) | copy-start | bytes 1572868
  122.0 3.6 %copy-start.16 = (s32[6,1024]{1,0:T(8,128)S(1)}, s32[6,1024]{1,0:T(8,128)}, u32[]{:S(2)}) copy-start(s32[6,1024]{1,0:T(8,128)} %param.13) | copy-start | bytes 73732
  125.5 5.1 %copy-start.57 = (f32[3,4]{1,0:T(4,128)S(1)}, f32[3,4]{1,0:T(4,128)}, u32[]{:S(2)}) copy-start(f32[3,4]{1,0:T(4,128)} %param.21) | copy-start | bytes 148
  125.5 5.3 %copy-start.15 = (f32[36,1024]{1,0:T(8,128)S(1)}, f32[36,1024]{1,0:T(8,128)}, u32[]{:S(2)}) copy-start(f32[36,1024]{1,0:T(8,128)} %param.14) | copy-start | bytes 442372
  130.7 20.9 %copy-start.51 = (f32[4]{0:T(128)}, f32[4]{0:T(128)S(1)}, u32[]{:S(2)}) copy-start(f32[4]{0:T(128)S(1)} %get-tuple-element.82) | copy-start | bytes 52
  130.7 20.9 %copy-start.53 = (f32[4]{0:T(128)}, f32[4]{0:T(128)S(1)}, u32[]{:S(2)}) copy-start(f32[4]{0:T(128)S(1)} %get-tuple-element.83) | copy-start | bytes 52
  130.7 20.9 %copy-start.55 = (f32[4]{0:T(128)}, f32[4]{0:T(128)S(1)}, u32[]{:S(2)}) copy-start(f32[4]{0:T(128)S(1)} %get-tuple-element.84) | copy-start | bytes 52
  133.9 31.4 %all-to-all-start = ((bf16[32,32,128]{2,1,0:T(8,128)(2,1)}), bf16[32,32,128]{2,1,0:T(8,128)(2,1)S(1)}, u32[]{:S(2)}, u32[]{:S(2)}) async-start(bf16[32,32,128]{2,1,0:T(8,128)(2,1)} %bitcast.2), calls=%async_computation | async-start | bytes 524288 | tf_op jit(solution)/shard_map/all_to_all | solution.py:108
  165.4 18.2 %copy-start.40 = (f32[1,1024]{1,0:T(1,128)S(1)}, f32[1,1024]{1,0:T(1,128)}, u32[]{:S(2)}) copy-start(f32[1,1024]{1,0:T(1,128)} %get-tuple-element.63) | copy-start | bytes 12292
  165.4 18.2 %copy-start.41 = (f32[1,1024]{1,0:T(1,128)S(1)}, f32[1,1024]{1,0:T(1,128)}, u32[]{:S(2)}) copy-start(f32[1,1024]{1,0:T(1,128)} %get-tuple-element.64) | copy-start | bytes 12292
  165.4 18.2 %copy-start.42 = (f32[1,1024]{1,0:T(1,128)S(1)}, f32[1,1024]{1,0:T(1,128)}, u32[]{:S(2)}) copy-start(f32[1,1024]{1,0:T(1,128)} %get-tuple-element.65) | copy-start | bytes 12292
  165.4 18.2 %copy-start.43 = (f32[1,1024]{1,0:T(1,128)S(1)}, f32[1,1024]{1,0:T(1,128)}, u32[]{:S(2)}) copy-start(f32[1,1024]{1,0:T(1,128)} %get-tuple-element.66) | copy-start | bytes 12292
  165.4 18.2 %copy-start.44 = (f32[1,1024]{1,0:T(1,128)S(1)}, f32[1,1024]{1,0:T(1,128)}, u32[]{:S(2)}) copy-start(f32[1,1024]{1,0:T(1,128)} %get-tuple-element.67) | copy-start | bytes 12292
  165.4 18.2 %copy-start.45 = (f32[1,1024]{1,0:T(1,128)S(1)}, f32[1,1024]{1,0:T(1,128)}, u32[]{:S(2)}) copy-start(f32[1,1024]{1,0:T(1,128)} %get-tuple-element.68) | copy-start | bytes 12292
  183.5 1.4 copy-start.34
  183.5 1.4 copy-start.35
  183.5 1.4 copy-start.36
  183.5 1.4 copy-start.37
  183.5 1.4 copy-start.38
  183.6 1.4 copy-start.39
  183.6 2.6 copy-start.25
  183.6 2.6 copy-start.26
  183.6 2.6 copy-start.27
  183.7 2.6 copy-start.46
  183.7 2.6 copy-start.47
  183.7 2.6 copy-start.48
  185.0 2.6 copy-start.28
  185.0 2.6 copy-start.29
  185.0 2.6 copy-start.30
  185.0 2.6 copy-start.31
  185.0 2.6 copy-start.32
  185.0 2.6 copy-start.33
  186.3 2.6 copy-start.20
  186.3 2.6 copy-start.21
  186.3 2.6 copy-start.22
  186.3 2.6 copy-start.23
  186.4 2.6 copy-start.24
  191.4 1.6 copy-start.17
  193.0 39.7 %copy-start.3 = (f32[384,1,128]{2,1,0:T(1,128)S(1)}, f32[384,1,128]{2,1,0:T(1,128)}, u32[]{:S(2)}) copy-start(f32[384,1,128]{2,1,0:T(1,128)} %get-tuple-element.16) | copy-start | bytes 589828
  193.0 39.7 %copy-start.4 = (f32[384,1,128]{2,1,0:T(1,128)S(1)}, f32[384,1,128]{2,1,0:T(1,128)}, u32[]{:S(2)}) copy-start(f32[384,1,128]{2,1,0:T(1,128)} %get-tuple-element.18) | copy-start | bytes 589828
  227.0 9.2 %copy-start = (f32[3072,128]{1,0:T(8,128)}, f32[3072,128]{1,0:T(8,128)S(1)}, u32[]{:S(2)}) copy-start(f32[3072,128]{1,0:T(8,128)S(1)} %scatter_custom_fusion) | copy-start | bytes 4718596
  227.0 7.5 %copy-start.2 = (f32[384,1,128]{2,1,0:T(1,128)S(1)}, f32[384,1,128]{2,1,0:T(1,128)}, u32[]{:S(2)}) copy-start(f32[384,1,128]{2,1,0:T(1,128)} %get-tuple-element.17) | copy-start | bytes 589828
  227.0 7.5 %copy-start.8 = (f32[384,1,128]{2,1,0:T(1,128)S(1)}, f32[384,1,128]{2,1,0:T(1,128)}, u32[]{:S(2)}) copy-start(f32[384,1,128]{2,1,0:T(1,128)} %get-tuple-element.20) | copy-start | bytes 589828
  227.0 7.5 %copy-start.9 = (f32[384,1,128]{2,1,0:T(1,128)S(1)}, f32[384,1,128]{2,1,0:T(1,128)}, u32[]{:S(2)}) copy-start(f32[384,1,128]{2,1,0:T(1,128)} %get-tuple-element.22) | copy-start | bytes 589828
  227.8 8.4 %copy-start.5 = (f32[384,1,128]{2,1,0:T(1,128)S(1)}, f32[384,1,128]{2,1,0:T(1,128)}, u32[]{:S(2)}) copy-start(f32[384,1,128]{2,1,0:T(1,128)} %get-tuple-element.26) | copy-start | bytes 589828
  227.8 8.4 %copy-start.6 = (f32[384,1,128]{2,1,0:T(1,128)S(1)}, f32[384,1,128]{2,1,0:T(1,128)}, u32[]{:S(2)}) copy-start(f32[384,1,128]{2,1,0:T(1,128)} %get-tuple-element.27) | copy-start | bytes 589828
  227.8 8.4 %copy-start.7 = (f32[384,1,128]{2,1,0:T(1,128)S(1)}, f32[384,1,128]{2,1,0:T(1,128)}, u32[]{:S(2)}) copy-start(f32[384,1,128]{2,1,0:T(1,128)} %get-tuple-element.28) | copy-start | bytes 589828
  227.8 8.4 %copy-start.52 = (f32[4]{0:T(128)S(1)}, f32[4]{0:T(128)}, u32[]{:S(2)}) copy-start(f32[4]{0:T(128)} %copy-done.51) | copy-start | bytes 52
  227.8 8.4 %copy-start.54 = (f32[4]{0:T(128)S(1)}, f32[4]{0:T(128)}, u32[]{:S(2)}) copy-start(f32[4]{0:T(128)} %copy-done.53) | copy-start | bytes 52
  227.8 8.4 %copy-start.56 = (f32[4]{0:T(128)S(1)}, f32[4]{0:T(128)}, u32[]{:S(2)}) copy-start(f32[4]{0:T(128)} %copy-done.55) | copy-start | bytes 52
  227.9 38.1 %all-to-all-start.1 = ((f32[32,32,128]{2,1,0:T(8,128)}), f32[32,32,128]{2,1,0:T(8,128)}, u32[]{:S(2)}, u32[]{:S(2)}) async-start(f32[32,32,128]{2,1,0:T(8,128)} %bitcast.52), calls=%async_computation.1 | async-start | bytes 1048576 | tf_op jit(solution)/shard_map/all_to_all | solution.py:123
  318.7 0.7 copy-start.49
  318.7 0.7 copy-start.50
  319.4 0.9 copy-start.11
  319.4 1.0 copy-start.12
  319.4 1.1 copy-start.13
  319.4 1.2 copy-start.14
  324.5 3.9 %copy-start.10 = (f32[8,64,64]{2,1,0:T(8,128)S(1)}, f32[8,64,64]{2,1,0:T(8,128)}, u32[]{:S(2)}) copy-start(f32[8,64,64]{2,1,0:T(8,128)} %copy.37) | copy-start | bytes 393220
Sparse Core Ops, SparseCore 0:
  94.5 86.0 all-gather.1
